TPU v7x, 32 devices: a whole 2x2x4 slice. The times are simulated.
32 devices in a mesh: row: 8 (over z, y), col: 4 (over x, core).
Axes of the slice: x: 2, y: 2, z: 4, core: 2. Of those that a mesh axis runs over, the one named last changes fastest.
Arguments:
- spectrum: float32 [2, 4096, 2048], P(None, 'row', 'col'), may hold values from -6 to 6
- pupil: float32 [2, 512, 512], replicated, may hold values from -4.2 to 4.2
- amplitudes: float32 [8, 4, 1, 512, 512], P('row', 'col'), may hold values from 0.1 to 3
- offsets: int32 [8, 4, 1, 2], P('row', 'col'), may hold values from 0 to 511, as said below
- counts: int32 [8, 4], P('row', 'col'), may hold values from 1 to 1, as said below
Outputs:
- recovered: float32 [2, 4096, 2048], P(None, 'row', 'col')
Inputs may be any that keep to these rules, and one draw needn't show every extreme that they name: `offsets`: offsets are corners inside the tile: the row below 512, the column below 512. `counts`: some device has all 1 slots live.
All inputs are finite; a program needn't handle non-finite values.
Results may differ from a plain program's by a relative error of at most 0.012.
Values sent between devices are 32-bit elements; how exact they have to be, the bound alone decides.
A program may use at most 128 MiB of HBM per device.

v0:
```python
import functools
import math

import jax
import jax.numpy as jnp
import numpy as np
from jax import lax
from jax.experimental import pallas as pl
from jax.experimental.pallas import tpu as pltpu
from jax.sharding import PartitionSpec as P

SWEEPS = 2
CHUNKS = 16
LAG = 4

step_size = 0.5
floor_value = 0.05

MESH = pl.DeviceIdType.MESH
BF16 = jnp.bfloat16
F32 = jnp.float32


def dft_tables(width):
    index = np.arange(width)
    angle = (index[:, None] * index[None, :] % width) * (2.0 * math.pi / width)
    scale = 1.0 / math.sqrt(width)
    return (
        jnp.asarray((np.cos(angle) * scale).astype(np.float32).astype(BF16)),
        jnp.asarray((np.sin(angle) * scale).astype(np.float32).astype(BF16)),
    )


def dot(a, b):
    return jnp.dot(a, b, preferred_element_type=F32)


def iota(shape, axis):
    return lax.broadcasted_iota(jnp.int32, shape, axis)


def kernel(
    n_row, n_col, place, count, spec, pupil_in, amps_in, cosine_in, sine_in, out,
    below1, right1, mix1, give1, got1, own, down1, above1, tile2,
    below2, right2, mix2, give2, got2, down2, above2,
    pup, fwd_right, fwd_left, back_right, back_left, f1, f2, hot, left_dr, send, recv, meta_sem,
    meta, pupil, amps, cosine, sine, load,
):
    width = spec.shape[1]
    size = width // CHUNKS
    r, c = lax.axis_index("row"), lax.axis_index("col")
    has_up, has_down = r > 0, r < n_row - 1
    has_left, has_right = c > 0, c < n_col - 1
    up = (lax.rem(r + n_row - 1, n_row), c)
    down = (lax.rem(r + 1, n_row), c)
    left = (r, lax.rem(c + n_col - 1, n_col))
    right = (r, lax.rem(c + 1, n_col))
    dr, dc = place[0], place[1]
    live = jnp.where(count[0] > 0, 1.0, 0.0)
    loads = [
        pltpu.make_async_copy(source, target, load.at[at])
        for at, (source, target) in enumerate(
            ((cosine_in, cosine), (sine_in, sine), (pupil_in, pupil), (amps_in, amps))
        )
    ]
    for copy in loads:
        copy.start()
    meta[...] = jnp.zeros_like(meta) + dr.astype(F32)

    def ds(k, block=size, base=0):
        return pl.ds(pl.multiple_of(base + k * block, 8), block)

    def flow(kind, src, dst, device):
        def copy(k):
            return pltpu.make_async_remote_copy(
                src_ref=src.at[:, ds(k), :], dst_ref=dst.at[:, ds(k), :],
                send_sem=send.at[kind, k], recv_sem=recv.at[kind, k],
                device_id=device, device_id_type=MESH,
            )
        return copy

    def each(body, count=CHUNKS):
        def step(k, carry):
            body(k)
            return carry
        lax.fori_loop(0, count, step, 0)

    neighbours = ((has_up, up), (has_down, down), (has_left, left), (has_right, right))
    barrier = pltpu.get_barrier_semaphore()
    for there, device in neighbours:
        @pl.when(there)
        def _():
            pl.semaphore_signal(barrier, inc=1, device_id=device, device_id_type=MESH)
    pl.semaphore_wait(barrier, sum(there.astype(jnp.int32) for there, _ in neighbours))

    up_flow = (flow(0, spec, below1, up), flow(3, tile2, below2, up))
    left_flow = (flow(1, mix1, right1, left), flow(2, mix2, right2, left))
    give_flow = (flow(4, give1, got1, right), flow(5, give2, got2, right))
    down_flow = (flow(6, down1, above1, down), flow(7, down2, above2, down))

    def meta_copy():
        return pltpu.make_async_remote_copy(
            src_ref=meta, dst_ref=left_dr, send_sem=meta_sem.at[0], recv_sem=meta_sem.at[1],
            device_id=right, device_id_type=MESH,
        )

    def first_sends(k):
        @pl.when(has_up)
        def _():
            up_flow[0](k).start()

    each(first_sends)

    @pl.when(jnp.logical_not(has_down))
    def _():
        for ref in (below1, below2):
            ref[...] = jnp.zeros_like(ref)

    @pl.when(jnp.logical_not(has_right))
    def _():
        for ref in (right1, right2):
            ref[...] = jnp.zeros_like(ref)

    @pl.when(jnp.logical_not(has_left))
    def _():
        for ref in (got1, got2, left_dr):
            ref[...] = jnp.zeros_like(ref)

    @pl.when(jnp.logical_not(has_up))
    def _():
        for ref in (above1, above2):
            ref[...] = jnp.zeros_like(ref)

    @pl.when(has_right)
    def _():
        meta_copy().start()

    block = 128
    shape = (block, width)

    def wrapped(value):
        return jnp.where(value >= width, value - width, value)

    def one_hot(mask):
        return jnp.where(mask, 1.0, 0.0).astype(BF16)

    def columns_of(i):
        at = iota(shape, 0) + i * block
        hot[0, ds(i, block)] = one_hot(iota(shape, 1) == wrapped(at + dr))
        hot[1, ds(i, block)] = one_hot(iota(shape, 1) == wrapped(at + dc))

    each(columns_of, width // block)

    def rows_hot(i, shift):
        return one_hot(iota(shape, 0) + i * block == wrapped(iota(shape, 1) + shift))

    def tables(i):
        top, low = ds(i, block), ds(i, block, width)
        near, far = pl.ds(0, width), pl.ds(width, width)

        def put(ref, cos, sin, top_sign, low_sign):
            ref[top, near] = cos.astype(BF16)
            ref[low, far] = cos.astype(BF16)
            ref[top, far] = (top_sign * sin).astype(BF16)
            ref[low, near] = (low_sign * sin).astype(BF16)

        hot_rows = rows_hot(i, dc)
        put(fwd_right, dot(hot_rows, cosine[...]), dot(hot_rows, sine[...]), 1.0, -1.0)
        hot_rows = rows_hot(i, dr)
        put(back_left, dot(hot_rows, cosine[...]), dot(hot_rows, sine[...]), 1.0, -1.0)
        cos, sin = cosine[ds(i, block)], sine[ds(i, block)]
        put(fwd_left, dot(cos, hot[0]), dot(sin, hot[0]), -1.0, 1.0)
        put(back_right, dot(cos, hot[1]), dot(sin, hot[1]), -1.0, 1.0)

    for copy in loads:
        copy.wait()
    each(tables, width // block)

    def three(value):
        high = value.astype(BF16)
        rest = value - high.astype(F32)
        middle = rest.astype(BF16)
        return high, middle, (rest - middle.astype(F32)).astype(BF16)

    for plane in range(2):
        def pupil_columns(i):
            parts = three(pupil[plane, ds(i, block)])
            moved = [dot(part, hot[1]) for part in parts]
            f1[ds(i, block)] = moved[0].astype(BF16)
            f1[ds(i, block, width)] = moved[1].astype(BF16)
            f2[ds(i, block)] = moved[2].astype(BF16)

        each(pupil_columns, width // block)

        def pupil_rows(i):
            hot_rows = rows_hot(i, dr)
            high = dot(hot_rows, f1[0:width])
            middle = dot(hot_rows, f1[width : 2 * width])
            pup[plane, ds(i, block)] = high + middle + dot(hot_rows, f2[0:width])

        each(pupil_rows, width // block)

    def masks(k):
        row = iota((size, width), 0) + k * size
        return row, row < dr, iota((size, width), 1) < dc

    def window(k, tile, below, right_tile):
        _, low, far = masks(k)
        rows = ds(k)
        planes = [
            jnp.where(
                far, right_tile[p, rows], jnp.where(low, below[p, rows], tile[p, rows])
            )
            for p in range(2)
        ]
        pr, pi = pup[0, rows], pup[1, rows]
        field_real = planes[0] * pr - planes[1] * pi
        field_imag = planes[0] * pi + planes[1] * pr
        both = jnp.concatenate([field_real, field_imag], axis=1).astype(BF16)
        first = dot(both, fwd_right[...])
        f1[rows] = first[:, :width].astype(BF16)
        f1[ds(k, size, width)] = first[:, width:].astype(BF16)

    wide = width // 2

    def middle(i):
        rows, low = ds(i, wide), ds(i, wide, width)
        wave = dot(jnp.concatenate([fwd_left[rows], fwd_left[low]], axis=0), f1[...])
        wave_real, wave_imag = wave[:wide], wave[wide:]
        magnitude = jnp.sqrt(wave_real * wave_real + wave_imag * wave_imag)
        keep = 1.0 - amps[rows] / jnp.maximum(magnitude, floor_value)
        both = jnp.concatenate([wave_real * keep, wave_imag * keep], axis=1).astype(BF16)
        first = dot(both, back_right[...])
        f2[rows] = first[:, :width].astype(BF16)
        f2[low] = first[:, width:].astype(BF16)

    tiles = (spec, tile2, out)
    for sweep in range(SWEEPS):
        tile, following = tiles[sweep], tiles[sweep + 1]
        below, right_tile, mix = ((below1, right1, mix1), (below2, right2, mix2))[sweep]
        give, got, lower, above = ((give1, got1, down1, above1), (give2, got2, down2, above2))[sweep]

        def relay(k):
            @pl.when(has_down)
            def _():
                up_flow[sweep](k).wait_recv()

            @pl.when(has_left)
            def _():
                rows = ds(k)
                row, _, _ = masks(k)
                left_low = row.astype(F32) < left_dr[0:1, :]
                for p in range(2):
                    mix[p, rows] = jnp.where(left_low, below[p, rows], tile[p, rows])
                left_flow[sweep](k).start()

        def consume(k):
            @pl.when(has_right)
            def _():
                left_flow[sweep](k).wait_recv()

            window(k, tile, below, right_tile)

        if sweep == 0:
            @pl.when(has_left)
            def _():
                meta_copy().wait_recv()

        relay(0)

        def gather(k):
            relay(k + 1)
            consume(k)

        each(gather, CHUNKS - 1)
        consume(CHUNKS - 1)
        each(middle, width // wide)

        def piece(k):
            _, _, far = masks(k)
            rows = ds(k)
            low = ds(k, size, width)
            back = dot(jnp.concatenate([back_left[rows], back_left[low]], axis=0), f2[...])
            back_real, back_imag = back[:size], back[size:]
            pr, pi = pup[0, rows], pup[1, rows]
            grads = (
                (back_real * pr + back_imag * pi) * live,
                (back_imag * pr - back_real * pi) * live,
            )
            for p in range(2):
                give[p, rows] = jnp.where(far, grads[p], 0.0)
                own[p, rows] = jnp.where(far, 0.0, grads[p])

            @pl.when(has_right)
            def _():
                give_flow[sweep](k).start()

        each(piece, LAG)

        def pass_down(k):
            row, low, _ = masks(k)
            rows = ds(k)

            @pl.when(has_left)
            def _():
                give_flow[sweep](k).wait_recv()

            left_low = row.astype(F32) < left_dr[0:1, :]
            for p in range(2):
                mine, theirs = own[p, rows], got[p, rows]
                lower[p, rows] = jnp.where(low, mine, 0.0) + jnp.where(left_low, theirs, 0.0)
                kept = jnp.where(low, 0.0, mine) + jnp.where(left_low, 0.0, theirs)
                following[p, rows] = tile[p, rows] - step_size * kept

            @pl.when(has_down)
            def _():
                down_flow[sweep](k).start()

        def both_ways(k):
            piece(k + LAG)
            pass_down(k)

        def last_down(k):
            pass_down(k + CHUNKS - LAG)

        each(both_ways, CHUNKS - LAG)
        each(last_down, LAG)

        def finish(k):
            rows = ds(k)

            @pl.when(has_up)
            def _():
                down_flow[sweep](k).wait_recv()

            for p in range(2):
                following[p, rows] = following[p, rows] - step_size * above[p, rows]
            if sweep + 1 < SWEEPS:
                @pl.when(has_up)
                def _():
                    up_flow[sweep + 1](k).start()

        each(finish)

    @pl.when(has_right)
    def _():
        meta_copy().wait_send()

    def sent(k):
        for sweep in range(SWEEPS):
            @pl.when(has_up)
            def _():
                up_flow[sweep](k).wait_send()

            @pl.when(has_left)
            def _():
                left_flow[sweep](k).wait_send()

            @pl.when(has_right)
            def _():
                give_flow[sweep](k).wait_send()

            @pl.when(has_down)
            def _():
                down_flow[sweep](k).wait_send()

    each(sent)


def on_device(n_row, n_col, spectrum, pupil, amplitudes, offsets, counts):
    width = pupil.shape[1]
    amps = amplitudes[0, 0, 0]
    place = offsets.reshape(-1)
    count = counts.reshape(-1)
    cosine, sine = dft_tables(width)
    plane = pltpu.VMEM((2, width, width), F32)
    table = pltpu.VMEM((2 * width, 2 * width), BF16)
    stage = pltpu.VMEM((2 * width, width), BF16)
    vmem = pl.BlockSpec(memory_space=pltpu.VMEM)
    return pl.pallas_call(
        functools.partial(kernel, n_row, n_col),
        out_shape=jax.ShapeDtypeStruct(spectrum.shape, F32),
        in_specs=[pl.BlockSpec(memory_space=pltpu.SMEM)] * 2
        + [vmem]
        + [pl.BlockSpec(memory_space=pltpu.MemorySpace.HBM)] * 4,
        out_specs=vmem,
        scratch_shapes=[plane] * 17
        + [table] * 4
        + [stage] * 2
        + [
            pltpu.VMEM((2, width, width), BF16),
            pltpu.VMEM((8, width), F32),
            pltpu.SemaphoreType.DMA((4 * SWEEPS, CHUNKS)),
            pltpu.SemaphoreType.DMA((4 * SWEEPS, CHUNKS)),
            pltpu.SemaphoreType.DMA((2,)),
            pltpu.VMEM((8, width), F32),
            plane,
            pltpu.VMEM((width, width), F32),
            pltpu.VMEM((width, width), BF16),
            pltpu.VMEM((width, width), BF16),
            pltpu.SemaphoreType.DMA((4,)),
        ],
        compiler_params=pltpu.CompilerParams(
            collective_id=0, has_side_effects=True, vmem_limit_bytes=66 * 1000 * 1000
        ),
    )(place, count, spectrum, pupil, amps, cosine, sine)


def solution(mesh):
    in_specs = (
        P(None, "row", "col"),
        P(),
        P("row", "col", None, None, None),
        P("row", "col", None, None),
        P("row", "col"),
    )
    return jax.shard_map(
        functools.partial(on_device, mesh.shape["row"], mesh.shape["col"]),
        mesh=mesh, in_specs=in_specs, out_specs=P(None, "row", "col"), check_vma=False,
    )
```

profile of v0, /device:TPU:25, one launch (start us, length us, event | category | flops | bytes accessed | tf_op | source)
XLA Modules:
  0.0 231.9 jit_solution(9318391037433648173)
XLA Ops:
  0.7 228.2 %shard_map.73 = f32[2,512,512]{2,1,0:T(8,128)} custom-call(s32[2]{0:T(128)} %bitcast.5, s32[1]{0:T(128)} %bitcast.3.count, f32[2,512,512]{2,1,0:T(8,128)} %spec.1, f32[2,512,512]{2,1,0:T(8,128)} %pupil_in.1, f32[512,512]{1,0:T(8,128)} %bitcast.4, bf16[512,512]{1,0:T(8,128)(2,1)} %constant.4.clone.cosine_in, bf16[512,512]{1,0:T(8,128)(2,1)} %constant.5.clone.sine_in), custom_call_target="tpu_custom_call" | custom-call | tf_op jit(solution)/shard_map/pallas_call | solution.py:380
  228.9 3.1 %copy.10 = f32[2,512,512]{2,1,0:T(8,128)} copy(f32[2,512,512]{2,1,0:T(8,128)} %shard_map.73) | data formatting | bytes 4194304
where the time goes:
time: 232 us
  Pallas kernels  228 us (98%)
  local copies, waits for them, and re-layouts  3.08 us (1%)
    pallas_call x1, Pallas kernels, on_device(): pl.pallas_call(functools.partial(kernel, n_row, n_col), out_shape=jax.Sha...  228 us

commit v1 on v0

v1 whole, which is shorter than its diff:
```python
import functools
import math

import jax
import jax.numpy as jnp
import numpy as np
from jax import lax
from jax.experimental import pallas as pl
from jax.experimental.pallas import tpu as pltpu
from jax.sharding import PartitionSpec as P

SWEEPS = 2
CHUNKS = 16
LAG = 3
RELAY = 2

step_size = 0.5
floor_value = 0.05

MESH = pl.DeviceIdType.MESH
BF16 = jnp.bfloat16
F32 = jnp.float32


def dft_tables(width):
    index = np.arange(width)
    angle = (index[:, None] * index[None, :] % width) * (2.0 * math.pi / width)
    scale = 1.0 / math.sqrt(width)
    return (
        jnp.asarray((np.cos(angle) * scale).astype(np.float32).astype(BF16)),
        jnp.asarray((np.sin(angle) * scale).astype(np.float32).astype(BF16)),
    )


def dot(a, b):
    return jnp.dot(a, b, preferred_element_type=F32)


def iota(shape, axis):
    return lax.broadcasted_iota(jnp.int32, shape, axis)


def kernel(
    n_row, n_col, place, count, spec, pupil_in, amps_in, cosine_in, sine_in, out,
    y1, z1, side1, mix1, win, grad1, from_left1, from_right1, give_p, got_p, give_z, got_z,
    total, from_left2, give_z2, got_z2, give_y2, got_y2,
    pup, fwd_right, fwd_left, back_right, back_left, f1, f2, hot,
    here, own, meta_l, meta_r, meta_p, meta_z,
    send, recv, meta_send, meta_recv, amps_sem,
    pupil, amps, cosine, sine, load,
):
    width = spec.shape[1]
    size = width // CHUNKS
    r, c = lax.axis_index("row"), lax.axis_index("col")
    parity = lax.rem(r, 2)
    mate = r + 1 - 2 * parity
    swapped = lax.rem(r // 2, 2) == 1
    home = jnp.where(swapped, mate, r)
    odd = lax.rem(home, 2) == 1
    even = jnp.logical_not(odd)
    has_z = jnp.where(odd, home < n_row - 1, home > 0)
    has_left, has_right = c > 0, c < n_col - 1
    left = (r, lax.rem(c + n_col - 1, n_col))
    right = (r, lax.rem(c + 1, n_col))
    partner = (mate, c)
    beyond = (lax.rem(jnp.where(odd, r + 2, r + n_row - 2), n_row), c)
    always = r >= 0
    side = jnp.where(odd, -1.0, 1.0)

    def both(*conditions):
        return functools.reduce(jnp.logical_and, conditions)

    def either(*conditions):
        return functools.reduce(jnp.logical_or, conditions)

    def when(condition, body):
        pl.when(condition)(body)

    stay = jnp.logical_not(swapped)
    loads = [
        pltpu.make_async_copy(source, target, load.at[at])
        for at, (source, target) in enumerate(
            ((cosine_in, cosine), (sine_in, sine), (pupil_in, pupil))
        )
    ]
    for copy in loads:
        copy.start()
    own_amps = pltpu.make_async_copy(amps_in, amps, load.at[3])
    when(stay, own_amps.start)
    for at, value in enumerate((place[0].astype(F32), place[1].astype(F32), jnp.where(count[0] > 0, 1.0, 0.0))):
        here[at] = jnp.zeros(here.shape[1:], F32) + value

    def ds(k, block=size, base=0):
        return pl.ds(pl.multiple_of(base + k * block, 8), block)

    def flow(kind, src, dst, device):
        def copy(k):
            return pltpu.make_async_remote_copy(
                src_ref=src.at[:, ds(k), :], dst_ref=dst.at[:, ds(k), :],
                send_sem=send.at[kind, k], recv_sem=recv.at[kind, k],
                device_id=device, device_id_type=MESH,
            )
        return copy

    def each(body, count=CHUNKS):
        def step(k, carry):
            body(k)
            return carry
        lax.fori_loop(0, count, step, 0)

    neighbours = ((always, partner), (has_z, beyond), (has_left, left), (has_right, right))
    barrier = pltpu.get_barrier_semaphore()
    for there, device in neighbours:
        @pl.when(there)
        def _():
            pl.semaphore_signal(barrier, inc=1, device_id=device, device_id_type=MESH)
    pl.semaphore_wait(barrier, sum(there.astype(jnp.int32) for there, _ in neighbours))

    def meta_copy(at, src, dst, device):
        return pltpu.make_async_remote_copy(
            src_ref=src, dst_ref=dst, send_sem=meta_send.at[at], recv_sem=meta_recv.at[at],
            device_id=device, device_id_type=MESH,
        )

    meta_swap = meta_copy(0, here, own, partner)
    meta_flows = (
        (meta_copy(1, own, meta_r, left), has_left, has_right),
        (meta_copy(2, own, meta_l, right), has_right, has_left),
        (meta_copy(3, own, meta_p, partner), always, always),
        (meta_copy(4, own, meta_z, beyond), has_z, has_z),
    )
    amps_flow = pltpu.make_async_remote_copy(
        src_ref=amps_in, dst_ref=amps, send_sem=amps_sem.at[0], recv_sem=amps_sem.at[1],
        device_id=partner, device_id_type=MESH,
    )

    y_in = (flow(0, spec, y1, partner), either(swapped, odd), either(swapped, even))
    z_from_spec = flow(1, spec, z1, beyond)
    z_from_y = flow(1, y1, z1, beyond)
    z_in = (z_from_spec, both(even, has_z), both(odd, has_z))
    mix_in = (flow(2, mix1, side1, left), has_left, has_right)
    grad_right = (flow(3, grad1, from_left1, right), has_right, has_left)
    grad_left = (flow(4, grad1, from_right1, left), has_left, has_right)
    over_p = (flow(5, give_p, got_p, partner), always, always)
    over_z = (flow(6, give_z, got_z, beyond), has_z, has_z)
    last_right = (flow(7, total, from_left2, right), has_right, has_left)
    z_out = (flow(8, give_z2, got_z2, beyond), both(odd, has_z), both(even, has_z))
    y_out = (flow(9, give_y2, got_y2, partner), either(swapped, even), either(swapped, odd))
    flows = (y_in, z_in, mix_in, grad_right, grad_left, over_p, over_z, last_right, z_out, y_out)

    def start(one, k):
        when(one[1], lambda: one[0](k).start())

    def arrive(one, k):
        when(one[2], lambda: one[0](k).wait_recv())

    when(swapped, meta_swap.start)

    def first_sends(k):
        start(y_in, k)
        when(both(stay, even, has_z), lambda: z_from_spec(k).start())

    each(first_sends)
    when(swapped, amps_flow.start)

    @pl.when(stay)
    def _():
        own[...] = here[...]

    def clear(*refs):
        for ref in refs:
            ref[...] = jnp.zeros_like(ref)

    when(jnp.logical_not(has_left), lambda: clear(from_left1, from_left2, meta_l))
    when(jnp.logical_not(has_right), lambda: clear(side1, from_right1, meta_r))
    when(jnp.logical_not(has_z), lambda: clear(z1, got_z, got_z2, meta_z))
    when(swapped, meta_swap.wait_recv)
    for copy, sends, _ in meta_flows:
        when(sends, copy.start)

    block = 128
    shape = (block, width)
    row_at, column_at, live = own[0, 0:1, :], own[1, 0:1, :], own[2, 0:1, :]

    def count_up(shape, axis):
        return iota(shape, axis).astype(F32)

    def wrapped(value):
        return jnp.where(value >= width, value - width, value)

    def one_hot(mask):
        return jnp.where(mask, 1.0, 0.0).astype(BF16)

    def columns_of(i):
        at = (iota(shape, 0) + i * block).astype(F32)
        hot[0, ds(i, block)] = one_hot(count_up(shape, 1) == wrapped(at + row_at))
        hot[1, ds(i, block)] = one_hot(count_up(shape, 1) == wrapped(at + column_at))

    each(columns_of, width // block)

    def rows_hot(i, shift):
        at = (iota(shape, 0) + i * block).astype(F32)
        return one_hot(at == wrapped(count_up(shape, 1) + shift))

    def tables(i):
        top, low = ds(i, block), ds(i, block, width)
        near, far = pl.ds(0, width), pl.ds(width, width)

        def put(ref, cos, sin, top_sign, low_sign):
            ref[top, near] = cos.astype(BF16)
            ref[low, far] = cos.astype(BF16)
            ref[top, far] = (top_sign * sin).astype(BF16)
            ref[low, near] = (low_sign * sin).astype(BF16)

        hot_rows = rows_hot(i, column_at)
        put(fwd_right, dot(hot_rows, cosine[...]), dot(hot_rows, sine[...]), 1.0, -1.0)
        hot_rows = rows_hot(i, row_at)
        put(back_left, dot(hot_rows, cosine[...]), dot(hot_rows, sine[...]), 1.0, -1.0)
        cos, sin = cosine[ds(i, block)], sine[ds(i, block)]
        put(fwd_left, dot(cos, hot[0]), dot(sin, hot[0]), -1.0, 1.0)
        put(back_right, dot(cos, hot[1]), dot(sin, hot[1]), -1.0, 1.0)

    for copy in loads:
        copy.wait()
    each(tables, width // block)

    def three(value):
        high = value.astype(BF16)
        rest = value - high.astype(F32)
        middle = rest.astype(BF16)
        return high, middle, (rest - middle.astype(F32)).astype(BF16)

    for plane in range(2):
        def pupil_columns(i):
            parts = three(pupil[plane, ds(i, block)])
            moved = [dot(part, hot[1]) for part in parts]
            f1[ds(i, block)] = moved[0].astype(BF16)
            f1[ds(i, block, width)] = moved[1].astype(BF16)
            f2[ds(i, block)] = moved[2].astype(BF16)

        each(pupil_columns, width // block)

        def pupil_rows(i):
            hot_rows = rows_hot(i, row_at)
            high = dot(hot_rows, f1[0:width])
            middle = dot(hot_rows, f1[width : 2 * width])
            pup[plane, ds(i, block)] = high + middle + dot(hot_rows, f2[0:width])

        each(pupil_rows, width // block)

    part = (size, width)

    def low_of(k, ref):
        return (iota(part, 0) + k * size).astype(F32) < ref[0, 0:1, :]

    def near_mate(k, ref):
        return side * ((iota(part, 0) + k * size).astype(F32) - ref[0, 0:1, :] + 0.5) < 0.0

    def far_of(ref):
        return count_up(part, 1) < ref[1, 0:1, :]

    def step_in(k, planes):
        rows = ds(k)
        pr, pi = pup[0, rows], pup[1, rows]
        field_real = planes[0] * pr - planes[1] * pi
        field_imag = planes[0] * pi + planes[1] * pr
        joined = jnp.concatenate([field_real, field_imag], axis=1).astype(BF16)
        first = dot(joined, fwd_right[...])
        f1[rows] = first[:, :width].astype(BF16)
        f1[ds(k, size, width)] = first[:, width:].astype(BF16)

    def tiles(k, p):
        rows = ds(k)
        near = jnp.where(swapped, y1[p, rows], spec[p, rows])
        mine = jnp.where(swapped, spec[p, rows], y1[p, rows])
        return near, jnp.where(odd, z1[p, rows], mine)

    def relay(k):
        arrive(y_in, k)
        when(both(swapped, even, has_z), lambda: z_from_y(k).start())

    def mix(k):
        arrive(z_in, k)
        rows = ds(k)
        own_low, left_low = low_of(k, own), low_of(k, meta_l)
        for p in range(2):
            near, below = tiles(k, p)
            win[p, rows] = jnp.where(own_low, below, near)
            mix1[p, rows] = jnp.where(left_low, below, near)
        start(mix_in, k)

    def consume(k):
        arrive(mix_in, k)
        rows, far = ds(k), far_of(own)
        planes = [jnp.where(far, side1[p, rows], win[p, rows]) for p in range(2)]
        for p in range(2):
            win[p, rows] = planes[p]
        step_in(k, planes)

    for copy, _, receives in meta_flows:
        when(receives, copy.wait_recv)

    relay(0)
    relay(1)
    mix(0)

    def gather(k):
        relay(k + 2)
        mix(k + 1)
        consume(k)

    each(gather, CHUNKS - 2)
    mix(CHUNKS - 1)
    consume(CHUNKS - 2)
    consume(CHUNKS - 1)

    wide = width // 2

    def middle(i):
        rows, low = ds(i, wide), ds(i, wide, width)
        wave = dot(jnp.concatenate([fwd_left[rows], fwd_left[low]], axis=0), f1[...])
        wave_real, wave_imag = wave[:wide], wave[wide:]
        magnitude = jnp.sqrt(wave_real * wave_real + wave_imag * wave_imag)
        keep = 1.0 - amps[rows] / jnp.maximum(magnitude, floor_value)
        joined = jnp.concatenate([wave_real * keep, wave_imag * keep], axis=1).astype(BF16)
        first = dot(joined, back_right[...])
        f2[rows] = first[:, :width].astype(BF16)
        f2[low] = first[:, width:].astype(BF16)

    def slope(k):
        rows, low = ds(k), ds(k, size, width)
        back = dot(jnp.concatenate([back_left[rows], back_left[low]], axis=0), f2[...])
        back_real, back_imag = back[:size], back[size:]
        pr, pi = pup[0, rows], pup[1, rows]
        return (
            (back_real * pr + back_imag * pi) * live,
            (back_imag * pr - back_real * pi) * live,
        )

    when(stay, own_amps.wait)
    when(swapped, amps_flow.wait_recv)
    each(middle, width // wide)

    def piece(k):
        rows = ds(k)
        grads = slope(k)
        for p in range(2):
            grad1[p, rows] = grads[p]
        start(grad_right, k)
        start(grad_left, k)

    def spread(k):
        arrive(grad_right, k)
        arrive(grad_left, k)
        rows = ds(k)
        mates, mates_l, mates_r = near_mate(k, own), near_mate(k, meta_l), near_mate(k, meta_r)
        far, far_l, far_r = far_of(own), far_of(meta_l), far_of(meta_r)
        far_p, far_z = far_of(meta_p), far_of(meta_z)
        for p in range(2):
            mine = grad1[p, rows]
            mine_near, mine_far = jnp.where(far, 0.0, mine), jnp.where(far, mine, 0.0)
            near = jnp.where(far_l, from_left1[p, rows], 0.0)
            past = jnp.where(far_r, 0.0, from_right1[p, rows])
            near_p, past_p = jnp.where(mates_l, near, 0.0), jnp.where(mates_r, past, 0.0)
            near_z, past_z = near - near_p, past - past_p
            give_p[p, rows] = jnp.where(
                far_p,
                jnp.where(mates, mine_far, 0.0) + past_p,
                jnp.where(mates, mine_near, 0.0) + near_p,
            )
            give_z[p, rows] = jnp.where(
                far_z,
                jnp.where(mates, 0.0, mine_far) + past_z,
                jnp.where(mates, 0.0, mine_near) + near_z,
            )
            beside = jnp.where(
                far, jnp.where(mates, past_p, past_z), jnp.where(mates, near_p, near_z)
            )
            win[p, rows] = win[p, rows] - step_size * (mine + beside)
        start(over_p, k)
        start(over_z, k)

    each(piece, LAG)

    def exchange(k):
        piece(k + LAG)
        spread(k)

    each(exchange, CHUNKS - LAG)
    each(lambda k: spread(k + CHUNKS - LAG), LAG)

    row_edge = jnp.where(both(odd, jnp.logical_not(has_z)), row_at, 0.0)
    column_edge = jnp.where(has_right, 0.0, column_at)

    def renew(k):
        arrive(over_p, k)
        arrive(over_z, k)
        rows, mates = ds(k), near_mate(k, own)
        inside = both(
            (iota(part, 0) + k * size).astype(F32) >= row_edge,
            count_up(part, 1) >= column_edge,
        )
        planes = [
            jnp.where(
                inside,
                win[p, rows] - step_size * jnp.where(mates, got_p[p, rows], got_z[p, rows]),
                0.0,
            )
            for p in range(2)
        ]
        step_in(k, planes)

    each(renew)
    each(middle, width // wide)

    def last_piece(k):
        rows = ds(k)
        grads = slope(k)
        for p in range(2):
            total[p, rows] = grad1[p, rows] + grads[p]
        start(last_right, k)

    def scatter(k):
        arrive(last_right, k)
        rows = ds(k)
        low, low_l, far, far_l = low_of(k, own), low_of(k, meta_l), far_of(own), far_of(meta_l)
        for p in range(2):
            mine = jnp.where(far, 0.0, total[p, rows])
            theirs = jnp.where(far_l, from_left2[p, rows], 0.0)
            mine_low, theirs_low = jnp.where(low, mine, 0.0), jnp.where(low_l, theirs, 0.0)
            lower = mine_low + theirs_low
            upper = (mine - mine_low) + (theirs - theirs_low)
            give_z2[p, rows] = lower
            give_y2[p, rows] = jnp.where(swapped, upper, lower)
            kept = jnp.where(swapped, jnp.where(odd, 0.0, lower), upper)
            out[p, rows] = spec[p, rows] - step_size * kept
        start(z_out, k)
        when(jnp.logical_not(both(swapped, even)), lambda: start(y_out, k))

    def pass_on(k):
        @pl.when(both(swapped, even))
        def _():
            arrive(z_out, k)
            rows = ds(k)
            for p in range(2):
                give_y2[p, rows] = give_y2[p, rows] + got_z2[p, rows]
            y_out[0](k).start()

    def finale(k):
        when(stay, lambda: arrive(z_out, k))
        arrive(y_out, k)
        rows = ds(k)
        for p in range(2):
            came = jnp.where(either(swapped, odd), got_y2[p, rows], got_z2[p, rows])
            out[p, rows] = out[p, rows] - step_size * came

    each(last_piece, LAG)

    def first_scatter(k):
        last_piece(k + LAG)
        scatter(k)

    each(first_scatter, RELAY)

    def steady(k):
        last_piece(k + LAG + RELAY)
        scatter(k + RELAY)
        pass_on(k)

    each(steady, CHUNKS - LAG - RELAY)

    def drain(k):
        scatter(k + CHUNKS - LAG)
        pass_on(k + CHUNKS - LAG - RELAY)

    each(drain, LAG)
    each(lambda k: pass_on(k + CHUNKS - RELAY), RELAY)
    each(finale)

    @pl.when(swapped)
    def _():
        meta_swap.wait_send()
        amps_flow.wait_send()

    for copy, sends, _ in meta_flows:
        when(sends, copy.wait_send)

    def sent(k):
        for one in flows:
            when(one[1], lambda: one[0](k).wait_send())

    each(sent)


def on_device(n_row, n_col, spectrum, pupil, amplitudes, offsets, counts):
    width = pupil.shape[1]
    amps = amplitudes[0, 0, 0]
    place = offsets.reshape(-1)
    count = counts.reshape(-1)
    cosine, sine = dft_tables(width)
    plane = pltpu.VMEM((2, width, width), F32)
    table = pltpu.VMEM((2 * width, 2 * width), BF16)
    stage = pltpu.VMEM((2 * width, width), BF16)
    note = pltpu.VMEM((3, 8, width), F32)
    vmem = pl.BlockSpec(memory_space=pltpu.VMEM)
    return pl.pallas_call(
        functools.partial(kernel, n_row, n_col),
        out_shape=jax.ShapeDtypeStruct(spectrum.shape, F32),
        in_specs=[pl.BlockSpec(memory_space=pltpu.SMEM)] * 2
        + [vmem]
        + [pl.BlockSpec(memory_space=pltpu.MemorySpace.HBM)] * 4,
        out_specs=vmem,
        scratch_shapes=[plane] * 19
        + [table] * 4
        + [stage] * 2
        + [pltpu.VMEM((2, width, width), BF16)]
        + [note] * 6
        + [
            pltpu.SemaphoreType.DMA((10, CHUNKS)),
            pltpu.SemaphoreType.DMA((10, CHUNKS)),
            pltpu.SemaphoreType.DMA((5,)),
            pltpu.SemaphoreType.DMA((5,)),
            pltpu.SemaphoreType.DMA((2,)),
            plane,
            pltpu.VMEM((width, width), F32),
            pltpu.VMEM((width, width), BF16),
            pltpu.VMEM((width, width), BF16),
            pltpu.SemaphoreType.DMA((4,)),
        ],
        compiler_params=pltpu.CompilerParams(
            collective_id=0, has_side_effects=True, vmem_limit_bytes=67 * 1000 * 1000
        ),
    )(place, count, spectrum, pupil, amps, cosine, sine)


def solution(mesh):
    in_specs = (
        P(None, "row", "col"),
        P(),
        P("row", "col", None, None, None),
        P("row", "col", None, None),
        P("row", "col"),
    )
    return jax.shard_map(
        functools.partial(on_device, mesh.shape["row"], mesh.shape["col"]),
        mesh=mesh, in_specs=in_specs, out_specs=P(None, "row", "col"), check_vma=False,
    )
```

time: 232 us -> 240 us (1.034)
  Pallas kernels: 228 us -> 236 us
    pallas_call x1, Pallas kernels: 228 us -> 236 us  [on_device(): pl.pallas_call(functools.partial(kernel, n_row, n_col), out_shape=jax.Sha...]
where the time goes in v1:
time: 240 us
  Pallas kernels  236 us (98%)
  local copies, waits for them, and re-layouts  3.08 us (1%)
    pallas_call x1, Pallas kernels, on_device(): pl.pallas_call(functools.partial(kernel, n_row, n_col), out_shape=jax.Sha...  236 us

profile of v1, /device:TPU:25, one launch (start us, length us, event | category | flops | bytes accessed | tf_op | source)
XLA Modules:
  0.0 239.8 jit_solution(12520985766400659658)
XLA Ops:
  0.7 236.1 %shard_map.73 = f32[2,512,512]{2,1,0:T(8,128)} custom-call(s32[2]{0:T(128)} %bitcast.5, s32[1]{0:T(128)} %bitcast.3.count, f32[2,512,512]{2,1,0:T(8,128)} %spec.1, f32[2,512,512]{2,1,0:T(8,128)} %pupil_in.1, f32[512,512]{1,0:T(8,128)} %bitcast.4, bf16[512,512]{1,0:T(8,128)(2,1)} %constant.4.clone.cosine_in, bf16[512,512]{1,0:T(8,128)(2,1)} %constant.5.clone.sine_in), custom_call_target="tpu_custom_call" | custom-call | tf_op jit(solution)/shard_map/pallas_call | solution.py:506
  236.8 3.1 %copy.10 = f32[2,512,512]{2,1,0:T(8,128)} copy(f32[2,512,512]{2,1,0:T(8,128)} %shard_map.73) | data formatting | bytes 4194304

commit v2 on v1

--- a/solution.py
+++ b/solution.py
@@ -11,7 +11,9 @@
 
 SWEEPS = 2
 CHUNKS = 16
+DEPTH = 2
 LAG = 3
+BACK = 3
 RELAY = 2
 
 step_size = 0.5
@@ -74,7 +76,10 @@
         return functools.reduce(jnp.logical_or, conditions)
 
     def when(condition, body):
-        pl.when(condition)(body)
+        if not isinstance(condition, bool):
+            pl.when(condition)(body)
+        elif condition:
+            body()
 
     stay = jnp.logical_not(swapped)
     loads = [
@@ -148,8 +153,12 @@
     y_out = (flow(9, give_y2, got_y2, partner), either(swapped, even), either(swapped, odd))
     flows = (y_in, z_in, mix_in, grad_right, grad_left, over_p, over_z, last_right, z_out, y_out)
 
+    def launch(copy, k):
+        when(k >= DEPTH, lambda: copy(k - DEPTH).wait_send())
+        copy(k).start()
+
     def start(one, k):
-        when(one[1], lambda: one[0](k).start())
+        when(one[1], lambda: launch(one[0], k))
 
     def arrive(one, k):
         when(one[2], lambda: one[0](k).wait_recv())
@@ -158,10 +167,10 @@
 
     def first_sends(k):
         start(y_in, k)
-        when(both(stay, even, has_z), lambda: z_from_spec(k).start())
-
-    each(first_sends)
-    when(swapped, amps_flow.start)
+        when(both(stay, even, has_z), lambda: launch(z_from_spec, k))
+
+    for k in range(DEPTH):
+        first_sends(k)
 
     @pl.when(stay)
     def _():
@@ -178,12 +187,53 @@
     for copy, sends, _ in meta_flows:
         when(sends, copy.start)
 
+    row_at, column_at, live = own[0, 0:1, :], own[1, 0:1, :], own[2, 0:1, :]
+
+    def count_up(shape, axis):
+        return iota(shape, axis).astype(F32)
+
+    part = (size, width)
+
+    def low_of(k, ref):
+        return (iota(part, 0) + k * size).astype(F32) < ref[0, 0:1, :]
+
+    def near_mate(k, ref):
+        return side * ((iota(part, 0) + k * size).astype(F32) - ref[0, 0:1, :] + 0.5) < 0.0
+
+    def far_of(ref):
+        return count_up(part, 1) < ref[1, 0:1, :]
+
+    def tiles(k, p):
+        rows = ds(k)
+        near = jnp.where(swapped, y1[p, rows], spec[p, rows])
+        mine = jnp.where(swapped, spec[p, rows], y1[p, rows])
+        return near, jnp.where(odd, z1[p, rows], mine)
+
+    def relay(k):
+        arrive(y_in, k)
+        when(both(swapped, even, has_z), lambda: launch(z_from_y, k))
+        when(k + DEPTH < CHUNKS, lambda: first_sends(k + DEPTH))
+        when(k + DEPTH == CHUNKS, lambda: when(swapped, amps_flow.start))
+
+    def mix(k):
+        arrive(z_in, k)
+        rows = ds(k)
+        own_low, left_low = low_of(k, own), low_of(k, meta_l)
+        for p in range(2):
+            near, below = tiles(k, p)
+            win[p, rows] = jnp.where(own_low, below, near)
+            mix1[p, rows] = jnp.where(left_low, below, near)
+        start(mix_in, k)
+
+    for copy, _, receives in meta_flows:
+        when(receives, copy.wait_recv)
+
+    def ahead(k):
+        when(k + 2 < CHUNKS, lambda: relay(k + 2))
+        mix(k)
+
     block = 128
     shape = (block, width)
-    row_at, column_at, live = own[0, 0:1, :], own[1, 0:1, :], own[2, 0:1, :]
-
-    def count_up(shape, axis):
-        return iota(shape, axis).astype(F32)
 
     def wrapped(value):
         return jnp.where(value >= width, value - width, value)
@@ -197,6 +247,9 @@
         hot[1, ds(i, block)] = one_hot(count_up(shape, 1) == wrapped(at + column_at))
 
     each(columns_of, width // block)
+    relay(0)
+    relay(1)
+    ahead(0)
 
     def rows_hot(i, shift):
         at = (iota(shape, 0) + i * block).astype(F32)
@@ -222,7 +275,18 @@
 
     for copy in loads:
         copy.wait()
-    each(tables, width // block)
+
+    def beside(body, first, every):
+        blocks = width // block
+
+        def step(i):
+            body(i)
+            when(lax.rem(i, every) == every - 1, lambda: ahead(first + i // every))
+
+        each(step, blocks)
+        return first + blocks // every
+
+    at = beside(tables, 1, 2)
 
     def three(value):
         high = value.astype(BF16)
@@ -238,7 +302,7 @@
             f1[ds(i, block, width)] = moved[1].astype(BF16)
             f2[ds(i, block)] = moved[2].astype(BF16)
 
-        each(pupil_columns, width // block)
+        at = beside(pupil_columns, at, 4)
 
         def pupil_rows(i):
             hot_rows = rows_hot(i, row_at)
@@ -246,18 +310,7 @@
             middle = dot(hot_rows, f1[width : 2 * width])
             pup[plane, ds(i, block)] = high + middle + dot(hot_rows, f2[0:width])
 
-        each(pupil_rows, width // block)
-
-    part = (size, width)
-
-    def low_of(k, ref):
-        return (iota(part, 0) + k * size).astype(F32) < ref[0, 0:1, :]
-
-    def near_mate(k, ref):
-        return side * ((iota(part, 0) + k * size).astype(F32) - ref[0, 0:1, :] + 0.5) < 0.0
-
-    def far_of(ref):
-        return count_up(part, 1) < ref[1, 0:1, :]
+        at = beside(pupil_rows, at, 4)
 
     def step_in(k, planes):
         rows = ds(k)
@@ -269,26 +322,6 @@
         f1[rows] = first[:, :width].astype(BF16)
         f1[ds(k, size, width)] = first[:, width:].astype(BF16)
 
-    def tiles(k, p):
-        rows = ds(k)
-        near = jnp.where(swapped, y1[p, rows], spec[p, rows])
-        mine = jnp.where(swapped, spec[p, rows], y1[p, rows])
-        return near, jnp.where(odd, z1[p, rows], mine)
-
-    def relay(k):
-        arrive(y_in, k)
-        when(both(swapped, even, has_z), lambda: z_from_y(k).start())
-
-    def mix(k):
-        arrive(z_in, k)
-        rows = ds(k)
-        own_low, left_low = low_of(k, own), low_of(k, meta_l)
-        for p in range(2):
-            near, below = tiles(k, p)
-            win[p, rows] = jnp.where(own_low, below, near)
-            mix1[p, rows] = jnp.where(left_low, below, near)
-        start(mix_in, k)
-
     def consume(k):
         arrive(mix_in, k)
         rows, far = ds(k), far_of(own)
@@ -297,22 +330,21 @@
             win[p, rows] = planes[p]
         step_in(k, planes)
 
-    for copy, _, receives in meta_flows:
-        when(receives, copy.wait_recv)
-
-    relay(0)
-    relay(1)
-    mix(0)
-
-    def gather(k):
-        relay(k + 2)
-        mix(k + 1)
-        consume(k)
-
-    each(gather, CHUNKS - 2)
-    mix(CHUNKS - 1)
-    consume(CHUNKS - 2)
-    consume(CHUNKS - 1)
+    late = CHUNKS - at
+    pairs = (CHUNKS - 2) - late
+
+    def catch_up(k):
+        ahead(at + k)
+        consume(2 * k)
+        consume(2 * k + 1)
+
+    def keep_up(k):
+        ahead(at + pairs + k)
+        consume(2 * pairs + k)
+
+    each(catch_up, pairs)
+    each(keep_up, late - pairs)
+    each(lambda k: consume(CHUNKS - 2 + k), 2)
 
     wide = width // 2
 
@@ -382,13 +414,6 @@
 
     each(piece, LAG)
 
-    def exchange(k):
-        piece(k + LAG)
-        spread(k)
-
-    each(exchange, CHUNKS - LAG)
-    each(lambda k: spread(k + CHUNKS - LAG), LAG)
-
     row_edge = jnp.where(both(odd, jnp.logical_not(has_z)), row_at, 0.0)
     column_edge = jnp.where(has_right, 0.0, column_at)
 
@@ -410,7 +435,13 @@
         ]
         step_in(k, planes)
 
-    each(renew)
+    def exchange(k):
+        when(k + LAG < CHUNKS, lambda: piece(k + LAG))
+        spread(k)
+        when(k >= BACK, lambda: renew(k - BACK))
+
+    each(exchange)
+    each(lambda k: renew(k + CHUNKS - BACK), BACK)
     each(middle, width // wide)
 
     def last_piece(k):
@@ -444,7 +475,7 @@
             rows = ds(k)
             for p in range(2):
                 give_y2[p, rows] = give_y2[p, rows] + got_z2[p, rows]
-            y_out[0](k).start()
+            launch(y_out[0], k)
 
     def finale(k):
         when(stay, lambda: arrive(z_out, k))
@@ -489,7 +520,7 @@
         for one in flows:
             when(one[1], lambda: one[0](k).wait_send())
 
-    each(sent)
+    each(lambda k: sent(k + CHUNKS - DEPTH), DEPTH)
 
 
 def on_device(n_row, n_col, spectrum, pupil, amplitudes, offsets, counts):

time: 240 us -> 194 us (0.81)
  Pallas kernels: 236 us -> 190 us
    pallas_call x1, Pallas kernels: 236 us -> 190 us  [on_device(): pl.pallas_call(functools.partial(kernel, n_row, n_col), out_shape=jax.Sha...]
where the time goes in v2:
time: 194 us; the launch traced here: 193 us
  Pallas kernels  190 us (98%)
  local copies, waits for them, and re-layouts  3.08 us (2%)
    pallas_call x1, Pallas kernels, on_device(): pl.pallas_call(functools.partial(kernel, n_row, n_col), out_shape=jax.Sha...  190 us

profile of v2, /device:TPU:25, one launch (start us, length us, event | category | flops | bytes accessed | tf_op | source)
XLA Modules:
  0.0 193.5 jit_solution(3790613521731155243)
XLA Ops:
  0.7 189.7 %shard_map.73 = f32[2,512,512]{2,1,0:T(8,128)} custom-call(s32[2]{0:T(128)} %bitcast.5, s32[1]{0:T(128)} %bitcast.3.count, f32[2,512,512]{2,1,0:T(8,128)} %spec.1, f32[2,512,512]{2,1,0:T(8,128)} %pupil_in.1, f32[512,512]{1,0:T(8,128)} %bitcast.4, bf16[512,512]{1,0:T(8,128)(2,1)} %constant.4.clone.cosine_in, bf16[512,512]{1,0:T(8,128)(2,1)} %constant.5.clone.sine_in), custom_call_target="tpu_custom_call" | custom-call | tf_op jit(solution)/shard_map/pallas_call | solution.py:537
  190.4 3.1 %copy.10 = f32[2,512,512]{2,1,0:T(8,128)} copy(f32[2,512,512]{2,1,0:T(8,128)} %shard_map.73) | data formatting | bytes 4194304

commit v3 on v2

--- a/solution.py
+++ b/solution.py
@@ -46,9 +46,9 @@
     n_row, n_col, place, count, spec, pupil_in, amps_in, cosine_in, sine_in, out,
     y1, z1, side1, mix1, win, grad1, from_left1, from_right1, give_p, got_p, give_z, got_z,
     total, from_left2, give_z2, got_z2, give_y2, got_y2,
-    pup, fwd_right, fwd_left, back_right, back_left, f1, f2, hot,
+    hop, pup, fwd_right, fwd_left, back_right, back_left, f1, f2, hot,
     here, own, meta_l, meta_r, meta_p, meta_z,
-    send, recv, meta_send, meta_recv, amps_sem,
+    send, recv, meta_send, meta_recv, amps_sem, first_amps, next_amps,
     pupil, amps, cosine, sine, load,
 ):
     width = spec.shape[1]
@@ -66,6 +66,9 @@
     right = (r, lax.rem(c + 1, n_col))
     partner = (mate, c)
     beyond = (lax.rem(jnp.where(odd, r + 2, r + n_row - 2), n_row), c)
+    has_cross = jnp.where(swapped, True, r + 2 < n_row)
+    cross = (lax.rem(jnp.where(swapped, r + n_row - 2, r + 2), n_row), c)
+    detour = lax.rem(c, 2) == 1
     always = r >= 0
     side = jnp.where(odd, -1.0, 1.0)
 
@@ -107,13 +110,25 @@
             )
         return copy
 
+    def flat(kind, src, dst, device):
+        def copy(k):
+            return pltpu.make_async_remote_copy(
+                src_ref=src.at[ds(k), :], dst_ref=dst.at[ds(k), :],
+                send_sem=send.at[kind, k], recv_sem=recv.at[kind, k],
+                device_id=device, device_id_type=MESH,
+            )
+        return copy
+
     def each(body, count=CHUNKS):
         def step(k, carry):
             body(k)
             return carry
         lax.fori_loop(0, count, step, 0)
 
-    neighbours = ((always, partner), (has_z, beyond), (has_left, left), (has_right, right))
+    neighbours = (
+        (always, partner), (has_z, beyond), (has_left, left), (has_right, right),
+        (both(parity == 0, has_cross), cross),
+    )
     barrier = pltpu.get_barrier_semaphore()
     for there, device in neighbours:
         @pl.when(there)
@@ -134,15 +149,24 @@
         (meta_copy(3, own, meta_p, partner), always, always),
         (meta_copy(4, own, meta_z, beyond), has_z, has_z),
     )
+
+    y_in = (flow(0, spec, y1, partner), either(swapped, odd), either(swapped, even))
+    direct = jnp.logical_not(detour)
+    z_in = (
+        flow(1, spec, z1, beyond), both(stay, even, has_z), both(odd, has_z, either(swapped, direct))
+    )
+    z_relay = (flow(1, y1, z1, beyond), both(swapped, even, has_z, direct), False)
+    hop_in = (flow(10, spec, hop, cross), both(swapped, odd, detour), both(stay, even, has_cross, detour))
+    z_hop = (flow(11, hop, z1, partner), both(stay, even, has_cross, detour), both(stay, odd, has_z, detour))
+    relays_amps = both(stay, detour, has_cross)
+    amps_1 = (flat(12, amps_in, first_amps, cross), both(swapped, detour), relays_amps)
+    amps_2 = (flat(13, first_amps, next_amps, partner), relays_amps, relays_amps)
+    amps_3 = (flat(14, next_amps, amps, cross), relays_amps, both(swapped, detour))
+    straight = both(swapped, direct)
     amps_flow = pltpu.make_async_remote_copy(
         src_ref=amps_in, dst_ref=amps, send_sem=amps_sem.at[0], recv_sem=amps_sem.at[1],
         device_id=partner, device_id_type=MESH,
     )
-
-    y_in = (flow(0, spec, y1, partner), either(swapped, odd), either(swapped, even))
-    z_from_spec = flow(1, spec, z1, beyond)
-    z_from_y = flow(1, y1, z1, beyond)
-    z_in = (z_from_spec, both(even, has_z), both(odd, has_z))
     mix_in = (flow(2, mix1, side1, left), has_left, has_right)
     grad_right = (flow(3, grad1, from_left1, right), has_right, has_left)
     grad_left = (flow(4, grad1, from_right1, left), has_left, has_right)
@@ -151,7 +175,8 @@
     last_right = (flow(7, total, from_left2, right), has_right, has_left)
     z_out = (flow(8, give_z2, got_z2, beyond), both(odd, has_z), both(even, has_z))
     y_out = (flow(9, give_y2, got_y2, partner), either(swapped, even), either(swapped, odd))
-    flows = (y_in, z_in, mix_in, grad_right, grad_left, over_p, over_z, last_right, z_out, y_out)
+    flows = (y_in, z_in, mix_in, grad_right, grad_left, over_p, over_z, last_right, z_out, y_out,
+             z_relay, hop_in, z_hop, amps_1, amps_2, amps_3)
 
     def launch(copy, k):
         when(k >= DEPTH, lambda: copy(k - DEPTH).wait_send())
@@ -166,11 +191,13 @@
     when(swapped, meta_swap.start)
 
     def first_sends(k):
-        start(y_in, k)
-        when(both(stay, even, has_z), lambda: launch(z_from_spec, k))
+        for one in (y_in, z_in, hop_in):
+            start(one, k)
 
     for k in range(DEPTH):
         first_sends(k)
+    for k in range(DEPTH):
+        start(amps_1, k)
 
     @pl.when(stay)
     def _():
@@ -211,12 +238,14 @@
 
     def relay(k):
         arrive(y_in, k)
-        when(both(swapped, even, has_z), lambda: launch(z_from_y, k))
+        start(z_relay, k)
+        arrive(hop_in, k)
+        start(z_hop, k)
         when(k + DEPTH < CHUNKS, lambda: first_sends(k + DEPTH))
-        when(k + DEPTH == CHUNKS, lambda: when(swapped, amps_flow.start))
 
     def mix(k):
         arrive(z_in, k)
+        arrive(z_hop, k)
         rows = ds(k)
         own_low, left_low = low_of(k, own), low_of(k, meta_l)
         for p in range(2):
@@ -228,9 +257,21 @@
     for copy, _, receives in meta_flows:
         when(receives, copy.wait_recv)
 
+    def second(k):
+        arrive(amps_1, k)
+        start(amps_2, k)
+
+    def third(k):
+        arrive(amps_2, k)
+        start(amps_3, k)
+
     def ahead(k):
         when(k + 2 < CHUNKS, lambda: relay(k + 2))
         mix(k)
+        when(k + 4 < CHUNKS, lambda: start(amps_1, k + 4))
+        when(k + 2 < CHUNKS, lambda: second(k + 2))
+        third(k)
+        when(k == CHUNKS - 2, lambda: when(straight, amps_flow.start))
 
     block = 128
     shape = (block, width)
@@ -249,6 +290,10 @@
     each(columns_of, width // block)
     relay(0)
     relay(1)
+    for k in range(DEPTH, 4):
+        start(amps_1, k)
+    second(0)
+    second(1)
     ahead(0)
 
     def rows_hot(i, shift):
@@ -370,7 +415,9 @@
         )
 
     when(stay, own_amps.wait)
-    when(swapped, amps_flow.wait_recv)
+
+    each(lambda k: arrive(amps_3, k))
+    when(straight, amps_flow.wait_recv)
     each(middle, width // wide)
 
     def piece(k):
@@ -508,10 +555,8 @@
     each(lambda k: pass_on(k + CHUNKS - RELAY), RELAY)
     each(finale)
 
-    @pl.when(swapped)
-    def _():
-        meta_swap.wait_send()
-        amps_flow.wait_send()
+    when(swapped, meta_swap.wait_send)
+    when(straight, amps_flow.wait_send)
 
     for copy, sends, _ in meta_flows:
         when(sends, copy.wait_send)
@@ -541,17 +586,19 @@
         + [vmem]
         + [pl.BlockSpec(memory_space=pltpu.MemorySpace.HBM)] * 4,
         out_specs=vmem,
-        scratch_shapes=[plane] * 19
+        scratch_shapes=[plane] * 20
         + [table] * 4
         + [stage] * 2
         + [pltpu.VMEM((2, width, width), BF16)]
         + [note] * 6
         + [
-            pltpu.SemaphoreType.DMA((10, CHUNKS)),
-            pltpu.SemaphoreType.DMA((10, CHUNKS)),
+            pltpu.SemaphoreType.DMA((15, CHUNKS)),
+            pltpu.SemaphoreType.DMA((15, CHUNKS)),
             pltpu.SemaphoreType.DMA((5,)),
             pltpu.SemaphoreType.DMA((5,)),
             pltpu.SemaphoreType.DMA((2,)),
+            pltpu.VMEM((width, width), F32),
+            pltpu.VMEM((width, width), F32),
             plane,
             pltpu.VMEM((width, width), F32),
             pltpu.VMEM((width, width), BF16),

time: 194 us -> 187 us (0.964)
  Pallas kernels: 190 us -> 183 us
    pallas_call x1, Pallas kernels: 190 us -> 183 us  [on_device(): pl.pallas_call(functools.partial(kernel, n_row, n_col), out_shape=jax.Sha...]
where the time goes in v3:
time: 187 us
  Pallas kernels  183 us (98%)
  local copies, waits for them, and re-layouts  3.08 us (2%)
    pallas_call x1, Pallas kernels, on_device(): pl.pallas_call(functools.partial(kernel, n_row, n_col), out_shape=jax.Sha...  183 us

profile of v3, /device:TPU:25, one launch (start us, length us, event | category | flops | bytes accessed | tf_op | source)
XLA Modules:
  0.0 186.6 jit_solution(6737126313123672355)
XLA Ops:
  0.7 182.8 %shard_map.73 = f32[2,512,512]{2,1,0:T(8,128)} custom-call(s32[2]{0:T(128)} %bitcast.5, s32[1]{0:T(128)} %bitcast.3.count, f32[2,512,512]{2,1,0:T(8,128)} %spec.1, f32[2,512,512]{2,1,0:T(8,128)} %pupil_in.1, f32[512,512]{1,0:T(8,128)} %bitcast.4, bf16[512,512]{1,0:T(8,128)(2,1)} %constant.4.clone.cosine_in, bf16[512,512]{1,0:T(8,128)(2,1)} %constant.5.clone.sine_in), custom_call_target="tpu_custom_call" | custom-call | tf_op jit(solution)/shard_map/pallas_call | solution.py:582
  183.5 3.1 %copy.10 = f32[2,512,512]{2,1,0:T(8,128)} copy(f32[2,512,512]{2,1,0:T(8,128)} %shard_map.73) | data formatting | bytes 4194304

commit v4 on v3

--- a/solution.py
+++ b/solution.py
@@ -43,7 +43,8 @@
 
 
 def kernel(
-    n_row, n_col, place, count, spec, pupil_in, amps_in, cosine_in, sine_in, out,
+    n_row, n_col, place, count, spec_in, pupil_in, amps_in, cosine_in, sine_in, out_hbm,
+    spec, out, spec_sem, out_sem,
     y1, z1, side1, mix1, win, grad1, from_left1, from_right1, give_p, got_p, give_z, got_z,
     total, from_left2, give_z2, got_z2, give_y2, got_y2,
     hop, pup, fwd_right, fwd_left, back_right, back_left, f1, f2, hot,
@@ -85,6 +86,8 @@
             body()
 
     stay = jnp.logical_not(swapped)
+    spec_load = pltpu.make_async_copy(spec_in, spec, spec_sem.at[0])
+    spec_load.start()
     loads = [
         pltpu.make_async_copy(source, target, load.at[at])
         for at, (source, target) in enumerate(
@@ -194,6 +197,7 @@
         for one in (y_in, z_in, hop_in):
             start(one, k)
 
+    spec_load.wait()
     for k in range(DEPTH):
         first_sends(k)
     for k in range(DEPTH):
@@ -271,7 +275,7 @@
         when(k + 4 < CHUNKS, lambda: start(amps_1, k + 4))
         when(k + 2 < CHUNKS, lambda: second(k + 2))
         third(k)
-        when(k == CHUNKS - 2, lambda: when(straight, amps_flow.start))
+        when(k == CHUNKS - 5, lambda: when(straight, amps_flow.start))
 
     block = 128
     shape = (block, width)
@@ -393,16 +397,30 @@
 
     wide = width // 2
 
-    def middle(i):
+    def wave_of(i):
         rows, low = ds(i, wide), ds(i, wide, width)
         wave = dot(jnp.concatenate([fwd_left[rows], fwd_left[low]], axis=0), f1[...])
-        wave_real, wave_imag = wave[:wide], wave[wide:]
+        return wave[:wide], wave[wide:]
+
+    def misfit(i, wave_real, wave_imag):
+        rows, low = ds(i, wide), ds(i, wide, width)
         magnitude = jnp.sqrt(wave_real * wave_real + wave_imag * wave_imag)
         keep = 1.0 - amps[rows] / jnp.maximum(magnitude, floor_value)
         joined = jnp.concatenate([wave_real * keep, wave_imag * keep], axis=1).astype(BF16)
         first = dot(joined, back_right[...])
         f2[rows] = first[:, :width].astype(BF16)
         f2[low] = first[:, width:].astype(BF16)
+
+    def middle(i):
+        misfit(i, *wave_of(i))
+
+    def early_wave(i):
+        rows = ds(i, wide)
+        give_y2[0, rows], give_y2[1, rows] = wave_of(i)
+
+    def late_misfit(i):
+        rows = ds(i, wide)
+        misfit(i, give_y2[0, rows], give_y2[1, rows])
 
     def slope(k):
         rows, low = ds(k), ds(k, size, width)
@@ -414,11 +432,11 @@
             (back_imag * pr - back_real * pi) * live,
         )
 
+    each(early_wave, width // wide)
     when(stay, own_amps.wait)
-
     each(lambda k: arrive(amps_3, k))
     when(straight, amps_flow.wait_recv)
-    each(middle, width // wide)
+    each(late_misfit, width // wide)
 
     def piece(k):
         rows = ds(k)
@@ -524,6 +542,11 @@
                 give_y2[p, rows] = give_y2[p, rows] + got_z2[p, rows]
             launch(y_out[0], k)
 
+    def stored(k):
+        return pltpu.make_async_copy(
+            out.at[:, ds(k), :], out_hbm.at[:, ds(k), :], out_sem.at[k]
+        )
+
     def finale(k):
         when(stay, lambda: arrive(z_out, k))
         arrive(y_out, k)
@@ -531,6 +554,7 @@
         for p in range(2):
             came = jnp.where(either(swapped, odd), got_y2[p, rows], got_z2[p, rows])
             out[p, rows] = out[p, rows] - step_size * came
+        stored(k).start()
 
     each(last_piece, LAG)
 
@@ -555,6 +579,7 @@
     each(lambda k: pass_on(k + CHUNKS - RELAY), RELAY)
     each(finale)
 
+    each(lambda k: stored(k).wait())
     when(swapped, meta_swap.wait_send)
     when(straight, amps_flow.wait_send)
 
@@ -578,15 +603,15 @@
     table = pltpu.VMEM((2 * width, 2 * width), BF16)
     stage = pltpu.VMEM((2 * width, width), BF16)
     note = pltpu.VMEM((3, 8, width), F32)
-    vmem = pl.BlockSpec(memory_space=pltpu.VMEM)
+    hbm = pl.BlockSpec(memory_space=pltpu.MemorySpace.HBM)
     return pl.pallas_call(
         functools.partial(kernel, n_row, n_col),
         out_shape=jax.ShapeDtypeStruct(spectrum.shape, F32),
-        in_specs=[pl.BlockSpec(memory_space=pltpu.SMEM)] * 2
-        + [vmem]
-        + [pl.BlockSpec(memory_space=pltpu.MemorySpace.HBM)] * 4,
-        out_specs=vmem,
-        scratch_shapes=[plane] * 20
+        in_specs=[pl.BlockSpec(memory_space=pltpu.SMEM)] * 2 + [hbm] * 5,
+        out_specs=hbm,
+        scratch_shapes=[plane] * 2
+        + [pltpu.SemaphoreType.DMA((1,)), pltpu.SemaphoreType.DMA((CHUNKS,))]
+        + [plane] * 20
         + [table] * 4
         + [stage] * 2
         + [pltpu.VMEM((2, width, width), BF16)]

time: 187 us -> 182 us (0.973)
  Pallas kernels: 183 us -> 178 us
    pallas_call x1, Pallas kernels: 183 us -> 178 us  [on_device(): pl.pallas_call(functools.partial(kernel, n_row, n_col), out_shape=jax.Sha...]
where the time goes in v4:
time: 182 us
  Pallas kernels  178 us (98%)
  local copies, waits for them, and re-layouts  3.08 us (2%)
    pallas_call x1, Pallas kernels, on_device(): pl.pallas_call(functools.partial(kernel, n_row, n_col), out_shape=jax.Sha...  178 us

profile of v4, /device:TPU:25, one launch (start us, length us, event | category | flops | bytes accessed | tf_op | source)
XLA Modules:
  0.0 181.6 jit_solution(5286650344063139890)
XLA Ops:
  0.7 177.8 %shard_map.73 = f32[2,512,512]{2,1,0:T(8,128)} custom-call(s32[2]{0:T(128)} %bitcast.5, s32[1]{0:T(128)} %bitcast.3.count, f32[2,512,512]{2,1,0:T(8,128)} %spec_in.1, f32[2,512,512]{2,1,0:T(8,128)} %pupil_in.1, f32[512,512]{1,0:T(8,128)} %bitcast.4, bf16[512,512]{1,0:T(8,128)(2,1)} %constant.4.clone.cosine_in, bf16[512,512]{1,0:T(8,128)(2,1)} %constant.5.clone.sine_in), custom_call_target="tpu_custom_call" | custom-call | tf_op jit(solution)/shard_map/pallas_call | solution.py:607
  178.5 3.1 %copy.10 = f32[2,512,512]{2,1,0:T(8,128)} copy(f32[2,512,512]{2,1,0:T(8,128)} %shard_map.73) | data formatting | bytes 4194304
